TPU v7x, 32 devices: a whole 2x2x4 slice. The times are simulated.
32 devices in a mesh: band: 4 (over z), px: 4 (over x, core), py: 2 (over y).
Axes of the slice: x: 2, y: 2, z: 4, core: 2. Of those that a mesh axis runs over, the one named last changes fastest.
Arguments:
- orbitals: bfloat16 [4, 1024, 384], P('band', ('px', 'py')), may hold values from -0.01171875 to 0.01171875
- occupations: float32 [4], P('band'), may hold values from 0.2 to 2
- stick_map: int32 [2, 1024], P(None, 'px'), may hold values from 0 to 191, as said below
- core_density: float32 [192, 192, 192], P('py', 'px'), may hold values from 0.05 to 0.5
Outputs:
- potential: float32 [192, 192, 192], P('py', 'px')
- gradient: float32 [3, 192, 192, 192], P(None, 'py', 'px')
Inputs may be any that keep to these rules, and one draw needn't show every extreme that they name: `stick_map`: columns i * 128 * 2 to (i + 1) * 128 * 2 - 1 have x index from i * 48 to (i + 1) * 48 - 1; no two columns share a grid position.
All inputs are finite; a program needn't handle non-finite values.
Results may differ from a plain program's by a relative error of at most 0.0054.
Values may be sent and summed in bfloat16 or wider, within the bound.
No kernel may reach another device: no remote copies, remote signals or barrier semaphores. Data moves between devices by JAX's collectives and lax.ppermute only.
A program may use at most 128 MiB of HBM per device.

v0:
```python
import math
import jax
import jax.numpy as jnp
from jax import lax
from jax.sharding import PartitionSpec as P

SPACING = 0.25
PBE_KAPPA = 0.804
PBE_MU = 0.2195
SLATER_COEF = 0.75 * (3.0 / math.pi) ** (1.0 / 3.0)
REDUCED_SCALE = 4.0 * (3.0 * math.pi**2) ** (2.0 / 3.0)
HIGHEST_PREC = lax.Precision.HIGHEST


def complex_table(row_index, col_index, points, direction):
    product = row_index[:, None] * col_index[None, :] % points
    angles = 2.0 * math.pi / points * product.astype(jnp.float32)
    cosine = jnp.cos(angles)
    sine_part = direction * jnp.sin(angles)
    return jnp.stack([jnp.stack([cosine, sine_part], 1), jnp.stack([-sine_part, cosine], 1)], 0)


def freq_pair(positions, points):
    signed = jnp.where(positions <= points // 2, positions, positions - points).astype(jnp.float32)
    gradient_freq = jnp.where(positions == points // 2, 0.0, signed)
    return (signed, gradient_freq)


def swap_rows(values):
    return lax.all_to_all(values, "px", split_axis=1, concat_axis=0, tiled=True)


def swap_depth(values):
    moved = lax.all_to_all(values, ("band", "py"), split_axis=1, concat_axis=0, tiled=True)
    return moved


def exchange_part(density, fields):
    cube_root = jnp.cbrt(density)
    four_thirds = density * cube_root
    grad_square = fields[1] * fields[1] + fields[2] * fields[2] + fields[3] * fields[3]
    reduced = grad_square / (REDUCED_SCALE * four_thirds * four_thirds)
    denominator = 1.0 + PBE_MU * reduced / PBE_KAPPA
    enhance = 1.0 + PBE_KAPPA - PBE_KAPPA / denominator
    enhance_slope = PBE_MU / (denominator * denominator)
    potential = fields[0] - SLATER_COEF * cube_root * (
        4.0 / 3.0 * enhance - 8.0 / 3.0 * reduced * enhance_slope
    )
    return jnp.concatenate([potential[None], fields[1:]], 0)


def transform(rho_local, pieces, depth_index, px_index):
    zshare, y_rows, points = rho_local.shape
    rows_px = lax.axis_size("px")
    rows_py = lax.axis_size("py")
    xblock = points // rows_px
    kyblock = points // pieces
    zblock = zshare * (pieces // rows_py)
    every_index = jnp.arange(points, dtype=jnp.int32)
    forward = complex_table(every_index, every_index, points, -1.0)
    x_table = forward[0].reshape(points, 2, rows_px, xblock).transpose(0, 2, 1, 3)
    section_data = jnp.einsum("zyx,xbsk->ybzsk", rho_local, x_table, precision=HIGHEST_PREC)
    section_data = swap_rows(section_data.reshape(y_rows, rows_px, zshare * 2 * xblock))
    section_data = section_data.reshape(points, zshare, 2, xblock)
    y_table = forward.reshape(2, points, 2, pieces, kyblock)
    section_data = jnp.einsum("yzrx,rysdk->zdksx", section_data, y_table, precision=HIGHEST_PREC)
    section_data = swap_depth(section_data.reshape(zshare, pieces, kyblock * 2 * xblock))
    section_data = section_data.reshape(pieces * zshare, kyblock, 2, xblock)
    source = jnp.arange(pieces * zshare, dtype=jnp.int32)
    device = source // zshare
    within = source % zshare
    z_order = device % rows_py * zblock + device // rows_py * zshare + within
    z_table = complex_table(z_order, every_index, points, -1.0)
    spectrum = jnp.einsum("zyrx,rzsk->kysx", section_data, z_table, precision=HIGHEST_PREC)
    q_depth, g_depth = freq_pair(every_index, points)
    ky_index = depth_index * kyblock + jnp.arange(kyblock, dtype=jnp.int32)
    q_col, g_col = freq_pair(ky_index, points)
    kx_index = px_index * xblock + jnp.arange(xblock, dtype=jnp.int32)
    q_row, g_row = freq_pair(kx_index, points)
    wave_unit = 2.0 * math.pi / (points * SPACING)
    squared = wave_unit**2 * (
        q_depth[:, None, None] ** 2 + q_col[None, :, None] ** 2 + q_row[None, None, :] ** 2
    )
    hartree = jnp.where(squared > 0, 4.0 * math.pi / jnp.where(squared > 0, squared, 1.0), 0.0)
    wave_z = wave_unit * g_depth[:, None, None]
    wave_y = wave_unit * g_col[None, :, None]
    wave_x = wave_unit * g_row[None, None, :]
    real_part = spectrum[:, :, 0, :]
    imag_part = spectrum[:, :, 1, :]
    first_factor = hartree - wave_x
    packed = jnp.stack(
        [
            jnp.stack([first_factor * real_part, first_factor * imag_part], 2),
            jnp.stack(
                [-wave_z * real_part - wave_y * imag_part, wave_y * real_part - wave_z * imag_part],
                2,
            ),
        ],
        0,
    )
    inverse = complex_table(every_index, every_index, points, 1.0)
    zi_table = complex_table(every_index, z_order, points, 1.0).reshape(
        2, points, 2, pieces, zshare
    )
    section_data = jnp.einsum("fkyrx,rksdz->ydfzsx", packed, zi_table, precision=HIGHEST_PREC)
    section_data = swap_depth(section_data.reshape(kyblock, pieces, 2 * zshare * 2 * xblock))
    section_data = section_data.reshape(points, 2, zshare, 2, xblock)
    yi_table = inverse.reshape(2, points, 2, rows_px, y_rows)
    section_data = jnp.einsum("kfzrx,rksby->xbfzsy", section_data, yi_table, precision=HIGHEST_PREC)
    section_data = swap_rows(section_data.reshape(xblock, rows_px, 2 * zshare * 2 * y_rows))
    section_data = section_data.reshape(points, 2, zshare, 2, y_rows)
    fields = jnp.einsum("kfzry,rksx->fszyx", section_data, inverse, precision=HIGHEST_PREC)
    fields = fields * (1.0 / float(points) ** 3)
    return fields.reshape(4, zshare, y_rows, points)


def body(orbitals, occupations, stick_map, core_density):
    bands_here, columns_here, doubled = orbitals.shape
    points = doubled // 2
    rows_px = lax.axis_size("px")
    rows_py = lax.axis_size("py")
    groups = lax.axis_size("band")
    px_index = lax.axis_index("px")
    py_index = lax.axis_index("py")
    xblock = points // rows_px
    zblock = points // rows_py
    y_rows = points // rows_px
    every_index = jnp.arange(points, dtype=jnp.int32)
    inverse = complex_table(every_index, every_index, points, 1.0)
    z_table = (
        inverse.reshape(2, points, 2, rows_py, zblock)
        .transpose(0, 1, 3, 2, 4)
        .reshape(doubled, doubled)
    )
    columns = jnp.dot(
        orbitals.astype(jnp.float32).reshape(bands_here * columns_here, doubled),
        z_table,
        precision=HIGHEST_PREC,
    )
    columns = columns.astype(jnp.bfloat16).reshape(bands_here, columns_here, doubled)
    columns = lax.all_to_all(columns, "py", split_axis=2, concat_axis=1, tiled=True)
    slot_index = stick_map[1] * xblock + (stick_map[0] - px_index * xblock)
    plane_data = (
        jnp.zeros((bands_here, points * xblock, 2 * zblock), jnp.float32)
        .at[:, slot_index]
        .set(columns.astype(jnp.float32))
    )
    plane_data = plane_data.reshape(bands_here, points, xblock, 2, zblock)
    plane_data = jnp.einsum("byxrz,rysk->bkxsz", plane_data, inverse, precision=HIGHEST_PREC)
    plane_data = plane_data.astype(jnp.bfloat16).reshape(bands_here, points, xblock * 2 * zblock)
    plane_data = lax.all_to_all(plane_data, "px", split_axis=1, concat_axis=2, tiled=True)
    plane_data = plane_data.astype(jnp.float32).reshape(bands_here, y_rows, points, 2, zblock)
    orbital_values = jnp.einsum("byxrz,rxsk->bszyk", plane_data, inverse, precision=HIGHEST_PREC)
    density = jnp.einsum(
        "b,bszyk->zyk", occupations, orbital_values * orbital_values, precision=HIGHEST_PREC
    )
    zshare = zblock // groups
    band_index = lax.axis_index("band")
    shared_rows = lax.psum_scatter(density, "band", scatter_dimension=0, tiled=True)
    core_rows = lax.dynamic_slice_in_dim(core_density, band_index * zshare, zshare, 0)
    rho_local = shared_rows + core_rows
    fields = transform(rho_local, groups * rows_py, band_index * rows_py + py_index, px_index)
    results = lax.all_gather(exchange_part(rho_local, fields), "band", axis=1, tiled=True)
    return (results[0], results[1:4])


def solution(mesh):
    return jax.shard_map(
        body,
        mesh=mesh,
        in_specs=(P("band", ("px", "py"), None), P("band"), P(None, "px"), P("py", "px", None)),
        out_specs=(P("py", "px", None), P(None, "py", "px", None)),
        check_vma=False,
    )
```

profile of v0, /device:TPU:0, one launch (start us, length us, event | category | flops | bytes accessed | tf_op | source)
XLA Modules:
  0.0 1160.9 jit_solution(13728535052132577211)
XLA Ops:
  27.8 12.3 %reshape.807 = f32[192,48,2,96]{3,2,1,0:T(2,128)} reshape(f32[9216,192]{1,0:T(8,128)} %scatter_custom_fusion) | data formatting | bytes 14155776 | tf_op jit(solution)/shard_map/reshape.2
  40.1 14.2 %copy.140 = f32[192,48,2,96]{0,3,2,1:T(8,128)} copy(f32[192,48,2,96]{3,2,1,0:T(2,128)} %reshape.807) | data formatting | bytes 14155776 | tf_op jit(solution)/shard_map/reshape.2
  54.3 18.6 %fusion.5 = bf16[1,192,48,2,96]{1,4,2,3,0:T(8,128)(2,1)} fusion(f32[192,48,2,96]{0,3,2,1:T(8,128)} %copy.140, f32[1,192,2,192]{3,1,0,2:T(8,128)S(1)} %get-tuple-element.11, f32[1,192,2,192]{3,1,0,2:T(8,128)S(1)} %get-tuple-element.10), kind=kOutput, calls=%fused_computation.8 | convolution fusion | flops 8155643904 | bytes 11206656 | tf_op jit(solution)/shard_map/byxrz,rysk->bkxsz/dot_general | solution.py:149
  72.8 11.6 copy.141
  84.4 24.4 %reshape.857 = bf16[1,192,9216]{2,0,1:T(2,128)(2,1)} reshape(bf16[1,192,48,2,96]{4,3,2,1,0:T(2,128)(2,1)} %copy.141) | data formatting | bytes 7077888 | tf_op jit(solution)/shard_map/reshape | solution.py:150
  108.8 78.5 %reduce.4 = bf16[192,9216]{1,0:T(8,128)(2,1)} reduce(bf16[192,1,9216]{2,1,0:T(2,128)(2,1)} %bitcast.221, bf16[]{:T(256)} %broadcast.1309), dimensions={1}, to_apply=%bitcast.207.reduce_sub_computation | reduce | bytes 7077890
  198.3 40.5 %all-to-all-done.1 = bf16[4,2,221184]{2,1,0:T(2,128)(2,1)} async-done(((bf16[4,2,221184]{2,1,0:T(2,128)(2,1)}), bf16[4,2,221184]{2,1,0:T(2,128)(2,1)}, u32[]{:S(2)}, u32[]{:S(2)}) %all-to-all-start.1) | async-done | bytes 3538976 | tf_op jit(solution)/shard_map/all_to_all | solution.py:151
  254.0 14.9 %reshape.809 = bf16[48,192,2,96]{3,2,1,0:T(2,128)(2,1)} reshape(bf16[1,48,4,9216]{3,2,1,0:T(4,128)(2,1)} %copy.143) | data formatting | bytes 7077888 | tf_op jit(solution)/shard_map/reshape.5
  268.9 10.5 fusion.2
  289.7 84.4 %reduce-scatter.2.cloned.1.call-done = f32[24,48,192]{2,1,0:T(8,128)} async-done(((f32[96,48,192]{2,1,0:T(8,128)}), f32[24,48,192]{2,1,0:T(8,128)}) %reduce-scatter.2.cloned.1.call-update) | async-done | bytes 884752 | tf_op jit(solution)/shard_map/reduce_scatter | solution.py:159
  380.9 7.5 copy.147
  388.4 9.3 reshape.811
  402.4 21.2 %all-to-all-done.2 = f32[48,4,2304]{2,0,1:T(8,128)S(1)} async-done(((f32[48,4,2304]{2,0,1:T(8,128)}), f32[48,4,2304]{2,0,1:T(8,128)S(1)}, u32[]{:S(2)}, u32[]{:S(2)}) %all-to-all-start.2) | async-done | bytes 1769504 | tf_op jit(solution)/shard_map/all_to_all | solution.py:30
  423.6 8.6 reshape.812
  432.2 10.4 fusion.27
  448.4 9.7 reshape.858
  466.9 37.3 %all-to-all-done.3 = f32[24,8,2304]{2,0,1:T(8,128)S(1)} async-done(((f32[24,8,2304]{2,0,1:T(8,128)}), f32[24,8,2304]{2,0,1:T(8,128)S(1)}, u32[]{:S(2)}, u32[]{:S(2)}) %all-to-all-start.3) | async-done | bytes 1769504 | tf_op jit(solution)/shard_map/all_to_all | solution.py:34
  504.1 8.6 reshape.814
  525.6 15.9 %fusion.22 = f32[24,8,2,24,2,48]{5,3,0,2,1,4:T(8,128)S(1)} fusion(f32[1,192,24,2,48]{1,4,2,3,0:T(8,128)S(1)} %maximum_bitcast_fusion.5, f32[1,192,24,2,48]{1,4,2,3,0:T(8,128)S(1)} %maximum_bitcast_fusion.4, f32[1,192,1,8,24]{1,4,0,3,2:T(8,128)S(1)} %copy-done.4, f32[1,192,1,8,24]{1,4,0,3,2:T(8,128)S(1)} %copy-done.3, ...), kind=kOutput, calls=%fused_computation.28 | convolution fusion | flops 4078190592 | bytes 7520256 | tf_op jit(solution)/shard_map/fkyrx,rksdz->ydfzsx/dot_general | solution.py:105
  541.5 8.0 copy.189
  549.5 16.6 %reshape.859 = f32[24,8,4608]{2,0,1:T(8,128)} reshape(f32[24,8,2,24,2,48]{5,4,3,2,0,1:T(2,128)} %copy.189) | data formatting | bytes 7077888 | tf_op jit(solution)/shard_map/reshape | solution.py:106
  571.5 77.6 %all-to-all-done.4 = f32[24,8,4608]{2,0,1:T(8,128)} async-done(((f32[24,8,4608]{2,0,1:T(8,128)}), f32[24,8,4608]{2,0,1:T(8,128)}, u32[]{:S(2)}, u32[]{:S(2)}) %all-to-all-start.4) | async-done | bytes 3538976 | tf_op jit(solution)/shard_map/all_to_all | solution.py:34
  649.2 17.3 %reshape.816 = f32[192,2,24,2,48]{4,3,2,1,0:T(2,128)} reshape(f32[8,24,1,4608]{3,1,0,2:T(8,128)} %bitcast.63) | data formatting | bytes 7077888 | tf_op jit(solution)/shard_map/reshape | solution.py:107
  666.5 24.9 %fusion.19 = f32[48,4,2,24,2,48]{0,5,3,2,1,4:T(8,128)} fusion(f32[192,2,24,2,48,1,1]{4,3,2,1,0,6,5:T(2,128)} %bitcast.218, f32[1,192,1,4,48]{1,4,0,3,2:T(8,128)S(1)} %get-tuple-element.20, f32[1,192,1,4,48]{1,4,0,3,2:T(8,128)S(1)} %get-tuple-element.19, f32[1,192,1,4,48]{1,4,0,3,2:T(8,128)S(1)} %get-tuple-element.18), kind=kOutput, calls=%fused_computation.27 | convolution fusion | flops 4077305856 | bytes 7520256 | tf_op jit(solution)/shard_map/kfzrx,rksby->xbfzsy/dot_general | solution.py:109
  691.4 13.7 %copy.157 = f32[48,4,2,24,2,48]{5,4,3,2,0,1:T(2,128)} copy(f32[48,4,2,24,2,48]{0,5,3,2,1,4:T(8,128)} %fusion.19) | data formatting | bytes 7077888 | tf_op jit(solution)/shard_map/kfzrx,rksby->xbfzsy/transpose | solution.py:109
  705.1 16.6 %reshape.817 = f32[48,4,4608]{2,0,1:T(8,128)} reshape(f32[48,4,2,24,2,48]{5,4,3,2,0,1:T(2,128)} %copy.157) | data formatting | bytes 7077888 | tf_op jit(solution)/shard_map/reshape | solution.py:110
  721.7 46.9 %all_to_all.84 = f32[48,4,4608]{2,0,1:T(8,128)} all-to-all(f32[48,4,4608]{2,0,1:T(8,128)} %reshape.817), channel_id=1, replica_groups=mesh['band'=4,'px'=4,'py'=2] {'px'}, dimensions={1} | all-to-all | bytes 7077888 | tf_op jit(solution)/shard_map/all_to_all | solution.py:30
  768.6 17.1 %reshape.818 = f32[192,2,24,2,48]{4,3,2,1,0:T(2,128)} reshape(f32[4,48,1,4608]{3,1,0,2:T(8,128)} %bitcast.224) | data formatting | bytes 7077888 | tf_op jit(solution)/shard_map/reshape | solution.py:111
  785.7 13.2 %copy.158 = f32[192,2,24,2,48]{0,4,3,2,1:T(8,128)} copy(f32[192,2,24,2,48]{4,3,2,1,0:T(2,128)} %reshape.818) | data formatting | bytes 7077888 | tf_op jit(solution)/shard_map/reshape | solution.py:111
  798.9 10.3 fusion.9
  816.6 320.4 %all-gather.2.cloned.1.call-done = f32[4,96,48,192]{3,2,1,0:T(8,128)} async-done(((f32[4,24,48,192]{3,2,1,0:T(8,128)}), f32[4,96,48,192]{3,2,1,0:T(8,128)}) %all-gather.2.cloned.1.call-update) | async-done | bytes 14155792 | tf_op jit(solution)/shard_map/all_gather | solution.py:163
  1141.8 11.8 %slice.55 = f32[3,96,48,192]{3,2,1,0:T(8,128)} slice(f32[4,96,48,192]{3,2,1,0:T(8,128)} %all-gather.2.cloned.1.call-done), slice={[1:4], [0:96], [0:48], [0:192]} | slice | bytes 21233664 | tf_op jit(solution)/shard_map/slice | solution.py:164
  (74 shorter events, 112.7 us)
Async XLA Ops:
  7.2 2.2 copy-start
  8.1 10.4 copy-start.5
  12.6 8.6 all-to-all-start
  192.9 45.9 %all-to-all-start.1 = ((bf16[4,2,221184]{2,1,0:T(2,128)(2,1)}), bf16[4,2,221184]{2,1,0:T(2,128)(2,1)}, u32[]{:S(2)}, u32[]{:S(2)}) async-start(bf16[4,2,221184]{2,1,0:T(2,128)(2,1)} %reshape.864), calls=%async_computation.1 | async-start | bytes 7077888 | tf_op jit(solution)/shard_map/all_to_all | solution.py:151
  197.6 176.5 %reduce-scatter.2.cloned.1.call-start = ((), (), s32[]{:S(2)}) async-start(), calls=%async_computation.7 | async-start | bytes 5898240 | tf_op jit(solution)/shard_map/reduce_scatter | solution.py:159
  397.7 25.9 %all-to-all-start.2 = ((f32[48,4,2304]{2,0,1:T(8,128)}), f32[48,4,2304]{2,0,1:T(8,128)S(1)}, u32[]{:S(2)}, u32[]{:S(2)}) async-start(f32[48,4,2304]{2,0,1:T(8,128)} %reshape.811), calls=%async_computation.3 | async-start | bytes 3538944 | tf_op jit(solution)/shard_map/all_to_all | solution.py:30
  458.1 46.0 %all-to-all-start.3 = ((f32[24,8,2304]{2,0,1:T(8,128)}), f32[24,8,2304]{2,0,1:T(8,128)S(1)}, u32[]{:S(2)}, u32[]{:S(2)}) async-start(f32[24,8,2304]{2,0,1:T(8,128)} %reshape.858), calls=%async_computation.4 | async-start | bytes 3538944 | tf_op jit(solution)/shard_map/all_to_all | solution.py:34
  524.6 0.9 copy-start.3
  524.6 1.0 copy-start.4
  566.1 83.1 %all-to-all-start.4 = ((f32[24,8,4608]{2,0,1:T(8,128)}), f32[24,8,4608]{2,0,1:T(8,128)}, u32[]{:S(2)}, u32[]{:S(2)}) async-start(f32[24,8,4608]{2,0,1:T(8,128)} %reshape.859), calls=%async_computation.5 | async-start | bytes 7077888 | tf_op jit(solution)/shard_map/all_to_all | solution.py:34
  570.6 566.4 %all-gather.2.cloned.1.call-start = ((), (), s32[]{:S(2)}) async-start(), calls=%async_computation.8 | async-start | bytes 23592960 | tf_op jit(solution)/shard_map/all_gather | solution.py:163
  809.6 1.3 copy-start.2
  1141.8 11.8 %copy-start.1 = (bf16[1,128,384]{2,1,0:T(8,128)(2,1)S(1)}, bf16[1,128,384]{2,1,0:T(8,128)(2,1)}, u32[]{:S(2)}) copy-start(bf16[1,128,384]{2,1,0:T(8,128)(2,1)} %param.4) | copy-start | bytes 294916
Sparse Core Ops, SparseCore 0:
  288.9 85.1 reduce-scatter.1
  816.7 320.2 all-gather.1
where the time goes:
time: 1170 us; the launch traced here: 1160 us
  waiting for transfers between devices  584 us (50%)
  local copies, waits for them, and re-layouts  291 us (25%)
  matrix products  103 us (9%)
  other arithmetic  98.1 us (8%)
  blocking collectives  46.9 us (4%)
  starting transfers between devices  22.4 us (2%)
  between operations  15.5 us (1%)
    all_gather x1, waiting for transfers between devices, body(): lax.all_gather(exchange_part(rho_local, fields), 'band', axis=1, tiled=True)  320 us
    all_to_all x2, waiting for transfers between devices, swap_depth(): lax.all_to_all(values, ('band', 'py'), split_axis=1, concat_axis=0, tiled...  115 us
    reduce_scatter x1, waiting for transfers between devices, body(): lax.psum_scatter(density, 'band', scatter_dimension=0, tiled=True)  84.4 us
    unnamed x2, other arithmetic  79.7 us
    all_to_all x1, blocking collectives, swap_rows(): return lax.all_to_all(values, 'px', split_axis=1, concat_axis=0, tiled=True)  46.9 us
    another operation x3, local copies, waits for them, and re-layouts  41.4 us
    all_to_all x1, waiting for transfers between devices, body(): lax.all_to_all(plane_data, 'px', split_axis=1, concat_axis=2, tiled=True)  40.5 us
    reshape x2, local copies, waits for them, and re-layouts, transform(): section_data = section_data.reshape(points, 2, zshare, 2, y_rows)  30.3 us
  transfers between devices with their start and end apart: 7, of which 7 were waited for; matrix products, arithmetic and copies ran while one was open for 1% of the time, Pallas kernels for 0%

commit v1 on v0

--- a/solution.py
+++ b/solution.py
@@ -160,7 +160,7 @@
     core_rows = lax.dynamic_slice_in_dim(core_density, band_index * zshare, zshare, 0)
     rho_local = shared_rows + core_rows
     fields = transform(rho_local, groups * rows_py, band_index * rows_py + py_index, px_index)
-    results = lax.all_gather(exchange_part(rho_local, fields), "band", axis=1, tiled=True)
+    results = jnp.concatenate(lax.all_gather(exchange_part(rho_local, fields), "band"), axis=1)
     return (results[0], results[1:4])
 
 

time: 1170 us -> 1180 us (level)
    slice x1 -> x3, local copies, waits for them, and re-layouts: 11.8 us -> 28.1 us  [body(): return (results[0], results[1:4])]
where the time goes in v1:
time: 1180 us; the launch traced here: 1170 us
  waiting for transfers between devices  585 us (50%)
  local copies, waits for them, and re-layouts  302 us (26%)
  matrix products  103 us (9%)
  other arithmetic  98.1 us (8%)
  blocking collectives  46.9 us (4%)
  starting transfers between devices  22.4 us (2%)
  between operations  15.5 us (1%)
    all_gather x1, waiting for transfers between devices, body(): lax.all_gather(exchange_part(rho_local, fields), 'band')  321 us
    all_to_all x2, waiting for transfers between devices, swap_depth(): lax.all_to_all(values, ('band', 'py'), split_axis=1, concat_axis=0, tiled...  115 us
    reduce_scatter x1, waiting for transfers between devices, body(): lax.psum_scatter(density, 'band', scatter_dimension=0, tiled=True)  84.4 us
    unnamed x2, other arithmetic  79.7 us
    all_to_all x1, blocking collectives, swap_rows(): return lax.all_to_all(values, 'px', split_axis=1, concat_axis=0, tiled=True)  46.9 us
    another operation x3, local copies, waits for them, and re-layouts  41.4 us
    all_to_all x1, waiting for transfers between devices, body(): lax.all_to_all(plane_data, 'px', split_axis=1, concat_axis=2, tiled=True)  40.5 us
    reshape x2, local copies, waits for them, and re-layouts, transform(): section_data = section_data.reshape(points, 2, zshare, 2, y_rows)  30.3 us
  transfers between devices with their start and end apart: 7, of which 7 were waited for; matrix products, arithmetic and copies ran while one was open for 1% of the time, Pallas kernels for 0%

profile of v1, /device:TPU:0, one launch (start us, length us, event | category | flops | bytes accessed | tf_op | source)
XLA Modules:
  0.0 1173.2 jit_solution(14635793057027786476)
XLA Ops:
  27.8 12.3 %reshape.814 = f32[192,48,2,96]{3,2,1,0:T(2,128)} reshape(f32[9216,192]{1,0:T(8,128)} %scatter_custom_fusion) | data formatting | bytes 14155776 | tf_op jit(solution)/shard_map/reshape.2
  40.1 14.2 %copy.146 = f32[192,48,2,96]{0,3,2,1:T(8,128)} copy(f32[192,48,2,96]{3,2,1,0:T(2,128)} %reshape.814) | data formatting | bytes 14155776 | tf_op jit(solution)/shard_map/reshape.2
  54.3 18.6 %fusion.5 = bf16[1,192,48,2,96]{1,4,2,3,0:T(8,128)(2,1)} fusion(f32[192,48,2,96]{0,3,2,1:T(8,128)} %copy.146, f32[1,192,2,192]{3,1,0,2:T(8,128)S(1)} %get-tuple-element.11, f32[1,192,2,192]{3,1,0,2:T(8,128)S(1)} %get-tuple-element.10), kind=kOutput, calls=%fused_computation.8 | convolution fusion | flops 8155643904 | bytes 11206656 | tf_op jit(solution)/shard_map/byxrz,rysk->bkxsz/dot_general | solution.py:149
  72.8 11.6 copy.147
  84.4 24.4 %reshape.866 = bf16[1,192,9216]{2,0,1:T(2,128)(2,1)} reshape(bf16[1,192,48,2,96]{4,3,2,1,0:T(2,128)(2,1)} %copy.147) | data formatting | bytes 7077888 | tf_op jit(solution)/shard_map/reshape | solution.py:150
  108.8 78.5 %reduce.4 = bf16[192,9216]{1,0:T(8,128)(2,1)} reduce(bf16[192,1,9216]{2,1,0:T(2,128)(2,1)} %bitcast.224, bf16[]{:T(256)} %broadcast.1309), dimensions={1}, to_apply=%bitcast.210.reduce_sub_computation | reduce | bytes 7077890
  198.3 40.5 %all-to-all-done.1 = bf16[4,2,221184]{2,1,0:T(2,128)(2,1)} async-done(((bf16[4,2,221184]{2,1,0:T(2,128)(2,1)}), bf16[4,2,221184]{2,1,0:T(2,128)(2,1)}, u32[]{:S(2)}, u32[]{:S(2)}) %all-to-all-start.1) | async-done | bytes 3538976 | tf_op jit(solution)/shard_map/all_to_all | solution.py:151
  254.0 14.9 %reshape.816 = bf16[48,192,2,96]{3,2,1,0:T(2,128)(2,1)} reshape(bf16[1,48,4,9216]{3,2,1,0:T(4,128)(2,1)} %copy.149) | data formatting | bytes 7077888 | tf_op jit(solution)/shard_map/reshape.5
  268.9 10.5 fusion.2
  289.7 84.4 %reduce-scatter.2.cloned.1.call-done = f32[24,48,192]{2,1,0:T(8,128)} async-done(((f32[96,48,192]{2,1,0:T(8,128)}), f32[24,48,192]{2,1,0:T(8,128)}) %reduce-scatter.2.cloned.1.call-update) | async-done | bytes 884752 | tf_op jit(solution)/shard_map/reduce_scatter | solution.py:159
  388.4 9.3 reshape.818
  402.4 21.2 %all-to-all-done.2 = f32[48,4,2304]{2,0,1:T(8,128)S(1)} async-done(((f32[48,4,2304]{2,0,1:T(8,128)}), f32[48,4,2304]{2,0,1:T(8,128)S(1)}, u32[]{:S(2)}, u32[]{:S(2)}) %all-to-all-start.2) | async-done | bytes 1769504 | tf_op jit(solution)/shard_map/all_to_all | solution.py:30
  423.6 8.6 reshape.819
  432.2 10.4 fusion.27
  448.4 9.7 reshape.867
  466.9 37.3 %all-to-all-done.3 = f32[24,8,2304]{2,0,1:T(8,128)S(1)} async-done(((f32[24,8,2304]{2,0,1:T(8,128)}), f32[24,8,2304]{2,0,1:T(8,128)S(1)}, u32[]{:S(2)}, u32[]{:S(2)}) %all-to-all-start.3) | async-done | bytes 1769504 | tf_op jit(solution)/shard_map/all_to_all | solution.py:34
  504.1 8.6 reshape.821
  525.6 15.9 %fusion.22 = f32[24,8,2,24,2,48]{5,3,0,2,1,4:T(8,128)S(1)} fusion(f32[1,192,24,2,48]{1,4,2,3,0:T(8,128)S(1)} %maximum_bitcast_fusion.5, f32[1,192,24,2,48]{1,4,2,3,0:T(8,128)S(1)} %maximum_bitcast_fusion.4, f32[1,192,1,8,24]{1,4,0,3,2:T(8,128)S(1)} %copy-done.4, f32[1,192,1,8,24]{1,4,0,3,2:T(8,128)S(1)} %copy-done.3, ...), kind=kOutput, calls=%fused_computation.27 | convolution fusion | flops 4078190592 | bytes 7520256 | tf_op jit(solution)/shard_map/fkyrx,rksdz->ydfzsx/dot_general | solution.py:105
  541.5 8.0 copy.196
  549.5 16.6 %reshape.868 = f32[24,8,4608]{2,0,1:T(8,128)} reshape(f32[24,8,2,24,2,48]{5,4,3,2,0,1:T(2,128)} %copy.196) | data formatting | bytes 7077888 | tf_op jit(solution)/shard_map/reshape | solution.py:106
  571.5 77.6 %all-to-all-done.4 = f32[24,8,4608]{2,0,1:T(8,128)} async-done(((f32[24,8,4608]{2,0,1:T(8,128)}), f32[24,8,4608]{2,0,1:T(8,128)}, u32[]{:S(2)}, u32[]{:S(2)}) %all-to-all-start.4) | async-done | bytes 3538976 | tf_op jit(solution)/shard_map/all_to_all | solution.py:34
  649.2 17.3 %reshape.823 = f32[192,2,24,2,48]{4,3,2,1,0:T(2,128)} reshape(f32[8,24,1,4608]{3,1,0,2:T(8,128)} %bitcast.63) | data formatting | bytes 7077888 | tf_op jit(solution)/shard_map/reshape | solution.py:107
  666.5 24.9 %fusion.19 = f32[48,4,2,24,2,48]{0,5,3,2,1,4:T(8,128)} fusion(f32[192,2,24,2,48,1,1]{4,3,2,1,0,6,5:T(2,128)} %bitcast.221, f32[1,192,1,4,48]{1,4,0,3,2:T(8,128)S(1)} %get-tuple-element.20, f32[1,192,1,4,48]{1,4,0,3,2:T(8,128)S(1)} %get-tuple-element.19, f32[1,192,1,4,48]{1,4,0,3,2:T(8,128)S(1)} %get-tuple-element.18), kind=kOutput, calls=%fused_computation.26 | convolution fusion | flops 4077305856 | bytes 7520256 | tf_op jit(solution)/shard_map/kfzrx,rksby->xbfzsy/dot_general | solution.py:109
  691.4 13.7 %copy.163 = f32[48,4,2,24,2,48]{5,4,3,2,0,1:T(2,128)} copy(f32[48,4,2,24,2,48]{0,5,3,2,1,4:T(8,128)} %fusion.19) | data formatting | bytes 7077888 | tf_op jit(solution)/shard_map/kfzrx,rksby->xbfzsy/transpose | solution.py:109
  705.1 16.6 %reshape.824 = f32[48,4,4608]{2,0,1:T(8,128)} reshape(f32[48,4,2,24,2,48]{5,4,3,2,0,1:T(2,128)} %copy.163) | data formatting | bytes 7077888 | tf_op jit(solution)/shard_map/reshape | solution.py:110
  721.7 46.9 %all_to_all.84 = f32[48,4,4608]{2,0,1:T(8,128)} all-to-all(f32[48,4,4608]{2,0,1:T(8,128)} %reshape.824), channel_id=1, replica_groups=mesh['band'=4,'px'=4,'py'=2] {'px'}, dimensions={1} | all-to-all | bytes 7077888 | tf_op jit(solution)/shard_map/all_to_all | solution.py:30
  768.6 17.1 %reshape.825 = f32[192,2,24,2,48]{4,3,2,1,0:T(2,128)} reshape(f32[4,48,1,4608]{3,1,0,2:T(8,128)} %bitcast.230) | data formatting | bytes 7077888 | tf_op jit(solution)/shard_map/reshape | solution.py:111
  785.7 13.2 %copy.164 = f32[192,2,24,2,48]{0,4,3,2,1:T(8,128)} copy(f32[192,2,24,2,48]{4,3,2,1,0:T(2,128)} %reshape.825) | data formatting | bytes 7077888 | tf_op jit(solution)/shard_map/reshape | solution.py:111
  798.9 10.6 fusion.9
  816.9 320.8 %all-gather.3.cloned.1.call-done = f32[16,24,48,192]{3,2,1,0:T(8,128)} async-done(((f32[4,24,48,192]{3,2,1,0:T(8,128)}), f32[16,24,48,192]{3,2,1,0:T(8,128)}) %all-gather.3.cloned.1.call-update) | async-done | bytes 14155792 | tf_op jit(solution)/shard_map/all_gather | solution.py:163
  1142.6 11.4 slice.60
  1154.1 11.8 %copy.166 = f32[3,4,24,48,192]{4,3,2,1,0:T(8,128)} copy(f32[3,4,24,48,192]{4,3,2,0,1:T(8,128)} %slice.60) | data formatting | bytes 21233664 | tf_op jit(solution)/shard_map/slice | solution.py:164
  (75 shorter events, 120.2 us)
Async XLA Ops:
  7.2 2.2 copy-start
  8.1 10.4 copy-start.5
  12.6 8.6 all-to-all-start
  192.9 45.9 %all-to-all-start.1 = ((bf16[4,2,221184]{2,1,0:T(2,128)(2,1)}), bf16[4,2,221184]{2,1,0:T(2,128)(2,1)}, u32[]{:S(2)}, u32[]{:S(2)}) async-start(bf16[4,2,221184]{2,1,0:T(2,128)(2,1)} %reshape.873), calls=%async_computation.1 | async-start | bytes 7077888 | tf_op jit(solution)/shard_map/all_to_all | solution.py:151
  197.6 176.5 %reduce-scatter.2.cloned.1.call-start = ((), (), s32[]{:S(2)}) async-start(), calls=%async_computation.7 | async-start | bytes 5898240 | tf_op jit(solution)/shard_map/reduce_scatter | solution.py:159
  397.7 25.9 %all-to-all-start.2 = ((f32[48,4,2304]{2,0,1:T(8,128)}), f32[48,4,2304]{2,0,1:T(8,128)S(1)}, u32[]{:S(2)}, u32[]{:S(2)}) async-start(f32[48,4,2304]{2,0,1:T(8,128)} %reshape.818), calls=%async_computation.3 | async-start | bytes 3538944 | tf_op jit(solution)/shard_map/all_to_all | solution.py:30
  458.1 46.0 %all-to-all-start.3 = ((f32[24,8,2304]{2,0,1:T(8,128)}), f32[24,8,2304]{2,0,1:T(8,128)S(1)}, u32[]{:S(2)}, u32[]{:S(2)}) async-start(f32[24,8,2304]{2,0,1:T(8,128)} %reshape.867), calls=%async_computation.4 | async-start | bytes 3538944 | tf_op jit(solution)/shard_map/all_to_all | solution.py:34
  524.6 0.9 copy-start.3
  524.6 1.0 copy-start.4
  566.1 83.1 %all-to-all-start.4 = ((f32[24,8,4608]{2,0,1:T(8,128)}), f32[24,8,4608]{2,0,1:T(8,128)}, u32[]{:S(2)}, u32[]{:S(2)}) async-start(f32[24,8,4608]{2,0,1:T(8,128)} %reshape.868), calls=%async_computation.5 | async-start | bytes 7077888 | tf_op jit(solution)/shard_map/all_to_all | solution.py:34
  570.6 567.1 %all-gather.3.cloned.1.call-start = ((), (), s32[]{:S(2)}) async-start(), calls=%async_computation.8 | async-start | bytes 23592960 | tf_op jit(solution)/shard_map/all_gather | solution.py:163
  809.9 1.3 copy-start.2
  1154.1 11.8 %copy-start.1 = (bf16[1,128,384]{2,1,0:T(8,128)(2,1)S(1)}, bf16[1,128,384]{2,1,0:T(8,128)(2,1)}, u32[]{:S(2)}) copy-start(bf16[1,128,384]{2,1,0:T(8,128)(2,1)} %param.4) | copy-start | bytes 294916
Sparse Core Ops, SparseCore 0:
  288.9 85.1 reduce-scatter.1
  817.0 320.6 all-gather.2
